TPU v7x, 32 devices: a whole 2x2x4 slice. The times are simulated.
32 devices in a mesh: dp: 8 (over y, x, core), expert: 4 (over z).
Axes of the slice: x: 2, y: 2, z: 4, core: 2. Of those that a mesh axis runs over, the one named last changes fastest.
Arguments:
- tokens: bfloat16 [4096, 2048], P(('dp', 'expert')), may hold values from -6 to 6
- cotangent: bfloat16 [4096, 2048], P(('dp', 'expert')), may hold values from -6 to 6
- expert_ids: int32 [4096, 2], P(('dp', 'expert')), may hold values from 0 to 3, all different within a row; in each aligned block of 128 rows (0 to 127, 128 to 255, ...) at most 128 rows name the same one
- combine: float32 [4096, 2], P(('dp', 'expert')), may hold values from 0.1 to 1
- w_gate: bfloat16 [4, 2048, 768], P('expert'), may hold values from -0.125 to 0.125
- w_up: bfloat16 [4, 2048, 768], P('expert'), may hold values from -0.125 to 0.125
- w_down: bfloat16 [4, 768, 2048], P('expert'), may hold values from -0.21875 to 0.21875
Outputs:
- input_grad: bfloat16 [4096, 2048], P(('dp', 'expert'))
- combine_grad: float32 [4096, 2], P(('dp', 'expert'))
- gate_grad: bfloat16 [4, 2048, 768], P('expert', 'dp')
- up_grad: bfloat16 [4, 2048, 768], P('expert', 'dp')
- down_grad: bfloat16 [4, 768, 2048], P('expert', 'dp')
Inputs may be any that keep to these rules, and one draw needn't show every extreme that they name: `expert_ids`: each token names 2 different experts. In the rows of one device no expert is named by more than 128 tokens, and in some devices' rows some expert is named by exactly 128.
All inputs are finite; a program needn't handle non-finite values.
Results may differ from a plain program's by a relative error of at most 0.02.
Values may be sent and summed in bfloat16 or wider, within the bound.
A program may use at most 128 MiB of HBM per device.

v0:
```python
import jax
import jax.numpy as jnp
from jax import lax
from jax.sharding import PartitionSpec as P


def shards(tokens, cotangent, expert_ids, combine, w_gate, w_up, w_down):
    first = (((0,), (0,)), ((), ()))
    last = (((1,), (1,)), ((), ()))
    local = w_gate.shape[0]
    groups = lax.axis_size("expert")
    experts = local * groups
    rows, top = expert_ids.shape
    hidden_width = w_gate.shape[2]
    names = jnp.arange(experts, dtype=jnp.int32)
    hits = expert_ids[:, :, None] == names
    weight = jnp.sum(jnp.where(hits, combine[:, :, None], 0.0), axis=1)
    weight = lax.all_to_all(weight, "expert", split_axis=1, concat_axis=0, tiled=True)
    x = lax.all_gather(tokens, "expert", axis=0, tiled=True)
    dy = lax.all_gather(cotangent, "expert", axis=0, tiled=True)
    row_sum = 0.0
    combs, gates, ups, downs = ([], [], [], [])
    for i in range(local):
        w_g, w_u, w_d = (w_gate[i], w_up[i], w_down[i])
        gate = jnp.dot(x, w_g, preferred_element_type=jnp.float32)
        up = jnp.dot(x, w_u, preferred_element_type=jnp.float32)
        sig = jax.nn.sigmoid(gate)
        act = gate * sig
        hidden = (act * up).astype(jnp.bfloat16)
        scaled = (weight[:, i : i + 1] * dy.astype(jnp.float32)).astype(jnp.bfloat16)
        output = jnp.dot(hidden, w_d, preferred_element_type=jnp.float32)
        combs.append(jnp.sum(dy.astype(jnp.float32) * output, axis=1))
        hidden_grad = lax.dot_general(scaled, w_d, last, preferred_element_type=jnp.float32)
        gate_d = (hidden_grad * up * (sig * (1.0 + gate * (1.0 - sig)))).astype(jnp.bfloat16)
        up_d = (hidden_grad * act).astype(jnp.bfloat16)
        row = lax.dot_general(gate_d, w_g, last, preferred_element_type=jnp.float32)
        row = row + lax.dot_general(up_d, w_u, last, preferred_element_type=jnp.float32)
        row_sum = row_sum + row.astype(jnp.bfloat16).astype(jnp.float32)
        downs.append(lax.dot_general(hidden, scaled, first, preferred_element_type=jnp.float32))
        gates.append(lax.dot_general(x, gate_d, first, preferred_element_type=jnp.float32))
        ups.append(lax.dot_general(x, up_d, first, preferred_element_type=jnp.float32))

    def reduced(parts):
        return jnp.stack(
            [
                lax.psum_scatter(part.astype(jnp.bfloat16), "dp", scatter_dimension=0, tiled=True)
                for part in parts
            ]
        )

    down_grad = reduced(downs)
    gate_grad = reduced(gates)
    up_grad = reduced(ups)
    input_grad = lax.psum_scatter(
        row_sum.astype(jnp.bfloat16), "expert", scatter_dimension=0, tiled=True
    )
    comb = jnp.stack(combs)
    comb = lax.all_to_all(comb, "expert", split_axis=1, concat_axis=0, tiled=True)
    combine_grad = jnp.sum(jnp.where(hits, comb.T[:, None, :], 0.0), axis=2)
    return (input_grad, combine_grad, gate_grad, up_grad, down_grad)


def solution(mesh):
    by_token = P(("dp", "expert"), None)
    by_expert = P("expert", None, None)
    by_row = P("expert", "dp", None)
    return jax.shard_map(
        shards,
        mesh=mesh,
        in_specs=(by_token,) * 4 + (by_expert,) * 3,
        out_specs=(by_token, by_token, by_row, by_row, by_row),
        check_vma=False,
    )
```

profile of v0, /device:TPU:0, one launch (start us, length us, event | category | flops | bytes accessed | tf_op | source)
XLA Modules:
  0.0 329.0 jit_solution(15756444999730954706)
XLA Ops:
  7.2 0.0 copy-start
  7.2 0.0 all-gather.5.cloned.1.call-start
  7.2 0.7 all-gather.5.cloned.1.call-update
  7.9 0.0 all-gather.3.cloned.1.call-start
  8.0 0.7 all-gather.3.cloned.1.call-update
  8.7 0.0 reduce-scatter.9.cloned.1.call-start
  8.7 49.3 %all-gather.5.cloned.1.call-done = bf16[512,2048]{1,0:T(8,128)(2,1)} async-done(((bf16[128,2048]{1,0:T(8,128)(2,1)}), bf16[512,2048]{1,0:T(8,128)(2,1)}) %all-gather.5.cloned.1.call-update) | async-done | bytes 2097168 | tf_op jit(solution)/shard_map/all_gather | solution.py:19
  58.0 4.5 %fusion.4 = f32[512,768]{1,0:T(8,128)S(1)} fusion(bf16[512,2048]{1,0:T(8,128)(2,1)} %all-gather.5.cloned.1.call-done, bf16[1,2048,768]{2,1,0:T(8,128)(2,1)} %param.11), kind=kOutput, calls=%fused_computation.10 | convolution fusion | flops 1610612736 | bytes 6815744 | tf_op jit(solution)/shard_map/dot_general | solution.py:25
  62.4 0.0 copy-start.9
  62.4 1.2 copy-done.9
  63.6 0.0 copy-done
  63.6 0.0 copy-done.5
  63.6 3.2 multiply_convert_fusion
  66.9 37.2 %all-gather.3.cloned.1.call-done = bf16[512,2048]{1,0:T(8,128)(2,1)} async-done(((bf16[128,2048]{1,0:T(8,128)(2,1)}), bf16[512,2048]{1,0:T(8,128)(2,1)}) %all-gather.3.cloned.1.call-update) | async-done | bytes 2097168 | tf_op jit(solution)/shard_map/all_gather | solution.py:20
  104.0 0.0 copy-start.11
  104.1 4.8 %fusion.1 = f32[512]{0:T(512)S(1)} fusion(bf16[512,2048]{1,0:T(8,128)(2,1)} %all-gather.3.cloned.1.call-done, bf16[512,768]{1,0:T(8,128)(2,1)} %get-tuple-element.29, bf16[1,768,2048]{2,1,0:T(8,128)(2,1)} %param.13), kind=kOutput, calls=%fused_computation.3 | convolution fusion | flops 1613757952 | bytes 6031360 | tf_op jit(solution)/shard_map/dot_general | solution.py:31
  108.9 8.0 %all_to_all.32 = f32[1,4,128]{2,0,1:T(1,128)S(1)} all-to-all(f32[1,4,128]{2,0,1:T(1,128)S(1)} %bitcast.56), channel_id=1, replica_groups=mesh['dp'=8,'expert'=4] {'expert'}, dimensions={1} | all-to-all | bytes 4096 | tf_op jit(solution)/shard_map/all_to_all | solution.py:58
  116.9 0.0 copy-done.1
  116.9 0.0 copy-done.2
  116.9 0.6 select_reduce_fusion
  117.5 7.9 %all_to_all.33 = f32[128,4,1]{0,2,1:T(1,128)S(1)} all-to-all(f32[128,4,1]{0,2,1:T(1,128)S(1)} %bitcast.53), channel_id=1, replica_groups=mesh['dp'=8,'expert'=4] {'expert'}, dimensions={1} | all-to-all | bytes 4096 | tf_op jit(solution)/shard_map/all_to_all | solution.py:18
  125.4 0.0 copy-done.3
  125.4 0.0 copy-done.4
  125.4 0.0 copy-done.10
  125.4 0.0 copy-done.11
  125.4 0.0 copy-start.6
  125.4 3.3 multiply_convert_fusion.1
  128.7 0.9 copy-done.7
  129.6 0.0 copy-done.6
  129.6 3.5 %fusion.14 = bf16[2048,768]{0,1:T(8,128)(2,1)} fusion(bf16[512,768]{1,0:T(8,128)(2,1)S(1)} %get-tuple-element.27, bf16[512,2048]{1,0:T(8,128)(2,1)S(1)} %copy-done.6), kind=kOutput, calls=%fused_computation.20 | convolution fusion | flops 1612185600 | bytes 6029312 | tf_op jit(solution)/shard_map/dot_general | solution.py:41
  133.1 0.0 reduce-scatter.9.cloned.1.call-update
  133.1 0.0 reduce-scatter.7.cloned.1.call-start
  133.2 5.3 %fusion.13 = bf16[2048,768]{0,1:T(8,128)(2,1)} fusion(bf16[512,768]{1,0:T(8,128)(2,1)} %get-tuple-element.28, bf16[512,2048]{1,0:T(8,128)(2,1)} %all-gather.5.cloned.1.call-done), kind=kOutput, calls=%fused_computation.19 | convolution fusion | flops 1612185600 | bytes 6029312 | tf_op jit(solution)/shard_map/dot_general | solution.py:40
  138.5 0.0 reduce-scatter.7.cloned.1.call-update
  138.5 0.2 reduce-scatter.5.cloned.1.call-start
  138.7 0.0 copy-start.8
  138.7 4.3 %fusion.2 = f32[512,2048]{1,0:T(8,128)S(1)} fusion(bf16[512,768]{1,0:T(8,128)(2,1)} %get-tuple-element.28, bf16[1,2048,768]{2,1,0:T(8,128)(2,1)} %param.11), kind=kOutput, calls=%fused_computation.8 | convolution fusion | flops 1610612736 | bytes 8126464 | tf_op jit(solution)/shard_map/dot_general | solution.py:36
  143.1 3.3 add_convert_fusion
  146.3 0.0 reduce-scatter.5.cloned.1.call-update
  146.4 0.0 reduce-scatter.11.cloned.1.call-start
  146.4 5.5 %convolution_convert_fusion = bf16[768,2048]{1,0:T(8,128)(2,1)} fusion(bf16[512,768]{1,0:T(8,128)(2,1)} %get-tuple-element.29, bf16[512,2048]{1,0:T(8,128)(2,1)} %all-gather.3.cloned.1.call-done, f32[512]{0:T(512)S(1)} %bitcast.55), kind=kOutput, calls=%fused_computation.5 | convolution fusion | flops 1615331328 | bytes 6031360 | tf_op jit(solution)/shard_map/dot_general | solution.py:39
  151.9 0.0 reduce-scatter.11.cloned.1.call-update
  151.9 25.5 %reduce-scatter.9.cloned.1.call-done = bf16[256,768]{0,1:T(8,128)(2,1)} async-done(((bf16[2048,768]{0,1:T(8,128)(2,1)}), bf16[256,768]{0,1:T(8,128)(2,1)}) %reduce-scatter.9.cloned.1.call-update) | async-done | bytes 393232 | tf_op jit(solution)/shard_map/reduce_scatter | solution.py:46
  177.4 1.9 copy.30
  179.3 47.4 %reduce-scatter.7.cloned.1.call-done = bf16[256,768]{0,1:T(8,128)(2,1)} async-done(((bf16[2048,768]{0,1:T(8,128)(2,1)}), bf16[256,768]{0,1:T(8,128)(2,1)}) %reduce-scatter.7.cloned.1.call-update) | async-done | bytes 393232 | tf_op jit(solution)/shard_map/reduce_scatter | solution.py:46
  226.7 1.9 copy.29
  228.6 44.4 %reduce-scatter.5.cloned.1.call-done = bf16[128,2048]{1,0:T(8,128)(2,1)} async-done(((bf16[512,2048]{1,0:T(8,128)(2,1)}), bf16[128,2048]{1,0:T(8,128)(2,1)}) %reduce-scatter.5.cloned.1.call-update) | async-done | bytes 524304 | tf_op jit(solution)/shard_map/reduce_scatter | solution.py:54
  273.0 49.1 %reduce-scatter.11.cloned.1.call-done = bf16[96,2048]{1,0:T(8,128)(2,1)} async-done(((bf16[768,2048]{1,0:T(8,128)(2,1)}), bf16[96,2048]{1,0:T(8,128)(2,1)}) %reduce-scatter.11.cloned.1.call-update) | async-done | bytes 393232 | tf_op jit(solution)/shard_map/reduce_scatter | solution.py:46
  (8 shorter events, 0.0 us)
Async XLA Ops:
  7.2 56.4 %copy-start = (bf16[1,2048,768]{2,1,0:T(8,128)(2,1)S(1)}, bf16[1,2048,768]{2,1,0:T(8,128)(2,1)}, u32[]{:S(2)}) copy-start(bf16[1,2048,768]{2,1,0:T(8,128)(2,1)} %param.12) | copy-start | bytes 9437188
  7.2 50.8 %all-gather.5.cloned.1.call-start = ((), (), s32[]{:S(2)}) async-start(), calls=%async_computation.7 | async-start | bytes 2621440 | tf_op jit(solution)/shard_map/all_gather | solution.py:19
  7.9 96.1 %all-gather.3.cloned.1.call-start = ((), (), s32[]{:S(2)}) async-start(), calls=%async_computation.6 | async-start | bytes 2621440 | tf_op jit(solution)/shard_map/all_gather | solution.py:20
  8.7 168.7 %reduce-scatter.9.cloned.1.call-start = ((), (), s32[]{:S(2)}) async-start(), calls=%async_computation.10 | async-start | bytes 3538944 | tf_op jit(solution)/shard_map/reduce_scatter | solution.py:46
  58.0 5.6 %copy-start.5 = (bf16[512,2048]{1,0:T(8,128)(2,1)S(1)}, bf16[512,2048]{1,0:T(8,128)(2,1)}, u32[]{:S(2)}) copy-start(bf16[512,2048]{1,0:T(8,128)(2,1)} %all-gather.5.cloned.1.call-done) | copy-start | bytes 6291460
  62.4 1.2 copy-start.9
  104.0 12.9 %copy-start.1 = (s32[128,2]{0,1:T(2,128)S(1)}, s32[128,2]{0,1:T(2,128)}, u32[]{:S(2)}) copy-start(s32[128,2]{0,1:T(2,128)} %param.9) | copy-start | bytes 3076
  104.0 12.9 %copy-start.2 = (f32[128,2]{0,1:T(2,128)S(1)}, f32[128,2]{0,1:T(2,128)}, u32[]{:S(2)}) copy-start(f32[128,2]{0,1:T(2,128)} %param.10) | copy-start | bytes 3076
  104.0 21.3 %copy-start.3 = (bf16[1,768,2048]{2,1,0:T(8,128)(2,1)S(1)}, bf16[1,768,2048]{2,1,0:T(8,128)(2,1)}, u32[]{:S(2)}) copy-start(bf16[1,768,2048]{2,1,0:T(8,128)(2,1)} %param.13) | copy-start | bytes 9437188
  104.0 21.3 %copy-start.4 = (bf16[512,2048]{1,0:T(8,128)(2,1)S(1)}, bf16[512,2048]{1,0:T(8,128)(2,1)}, u32[]{:S(2)}) copy-start(bf16[512,2048]{1,0:T(8,128)(2,1)} %all-gather.3.cloned.1.call-done) | copy-start | bytes 6291460
  104.0 21.3 %copy-start.10 = (f32[512,768]{1,0:T(8,128)S(1)}, f32[512,768]{1,0:T(8,128)}, u32[]{:S(2)}) copy-start(f32[512,768]{1,0:T(8,128)} %copy-done.9) | copy-start | bytes 4718596
  104.0 21.3 %copy-start.11 = (f32[512,768]{1,0:T(8,128)S(1)}, f32[512,768]{1,0:T(8,128)}, u32[]{:S(2)}) copy-start(f32[512,768]{1,0:T(8,128)} %get-tuple-element.30) | copy-start | bytes 4718596
  125.4 4.2 %copy-start.6 = (bf16[512,2048]{1,0:T(8,128)(2,1)S(1)}, bf16[512,2048]{1,0:T(8,128)(2,1)}, u32[]{:S(2)}) copy-start(bf16[512,2048]{1,0:T(8,128)(2,1)} %all-gather.5.cloned.1.call-done) | copy-start | bytes 6291460
  128.7 0.9 copy-start.7
  133.1 93.6 %reduce-scatter.7.cloned.1.call-start = ((), (), s32[]{:S(2)}) async-start(), calls=%async_computation.9 | async-start | bytes 3538944 | tf_op jit(solution)/shard_map/reduce_scatter | solution.py:46
  138.5 134.5 %reduce-scatter.5.cloned.1.call-start = ((), (), s32[]{:S(2)}) async-start(), calls=%async_computation.8 | async-start | bytes 2621440 | tf_op jit(solution)/shard_map/reduce_scatter | solution.py:54
  138.7 4.3 %copy-start.8 = (bf16[512,768]{1,0:T(8,128)(2,1)S(1)}, bf16[512,768]{1,0:T(8,128)(2,1)}, u32[]{:S(2)}) copy-start(bf16[512,768]{1,0:T(8,128)(2,1)} %copy-done.7) | copy-start | bytes 2359300
  146.4 175.8 %reduce-scatter.11.cloned.1.call-start = ((), (), s32[]{:S(2)}) async-start(), calls=%async_computation.11 | async-start | bytes 3538944 | tf_op jit(solution)/shard_map/reduce_scatter | solution.py:46
Sparse Core Ops, SparseCore 0:
  9.6 48.3 all-gather.4
  59.5 44.4 all-gather.2
  133.2 44.0 reduce-scatter.8
  180.6 46.0 reduce-scatter.6
  229.4 43.5 reduce-scatter.4
  276.8 45.2 reduce-scatter.10
where the time goes:
time: 329 us
  waiting for transfers between devices  254 us (77%)
  matrix products  37.7 us (11%)
  blocking collectives  15.9 us (5%)
  between operations  14.2 us (4%)
  local copies, waits for them, and re-layouts  5.92 us (2%)
    reduce_scatter x3, waiting for transfers between devices, reduced(): lax.psum_scatter(part.astype(jnp.bfloat16), 'dp', scatter_dimension=0, ti...  122 us
    all_gather x1, waiting for transfers between devices, shards(): x = lax.all_gather(tokens, 'expert', axis=0, tiled=True)  49.3 us
    reduce_scatter x1, waiting for transfers between devices, shards(): lax.psum_scatter(row_sum.astype(jnp.bfloat16), 'expert', scatter_dimensio...  44.4 us
    all_gather x1, waiting for transfers between devices, shards(): dy = lax.all_gather(cotangent, 'expert', axis=0, tiled=True)  37.2 us
    all_to_all x1, blocking collectives, shards(): lax.all_to_all(comb, 'expert', split_axis=1, concat_axis=0, tiled=True)  8.03 us
    all_to_all x1, blocking collectives, shards(): lax.all_to_all(weight, 'expert', split_axis=1, concat_axis=0, tiled=True)  7.9 us
  transfers between devices with their start and end apart: 6, of which 6 were waited for; matrix products, arithmetic and copies ran while one was open for 9% of the time, Pallas kernels for 0%

commit v1 on v0

--- a/solution.py
+++ b/solution.py
@@ -2,6 +2,24 @@
 import jax.numpy as jnp
 from jax import lax
 from jax.sharding import PartitionSpec as P
+from jax.lax import axis_index, axis_size, ppermute
+
+
+def keys_play(view):
+    peer_axis = "expert"
+    n_parts = axis_size(peer_axis)
+    cards = [view]
+    dev_j = 0
+    while dev_j < n_parts - 1:
+        d_next = ppermute(
+            cards[-1], peer_axis, [(dev, (dev + 1) % n_parts) for dev in range(n_parts)]
+        )
+        cards.append(d_next)
+        dev_j += 1
+    a_now = jnp.concatenate(cards[::-1], axis=0)
+    s_next = axis_index(peer_axis)
+    spare = jnp.roll(a_now, (s_next + 1) * view.shape[0], axis=0)
+    return spare
 
 
 def shards(tokens, cotangent, expert_ids, combine, w_gate, w_up, w_down):
@@ -16,7 +34,7 @@
     hits = expert_ids[:, :, None] == names
     weight = jnp.sum(jnp.where(hits, combine[:, :, None], 0.0), axis=1)
     weight = lax.all_to_all(weight, "expert", split_axis=1, concat_axis=0, tiled=True)
-    x = lax.all_gather(tokens, "expert", axis=0, tiled=True)
+    x = keys_play(tokens)
     dy = lax.all_gather(cotangent, "expert", axis=0, tiled=True)
     row_sum = 0.0
     combs, gates, ups, downs = ([], [], [], [])

time: 329 us -> 315 us (0.957)
  waiting for transfers between devices: 254 us -> 240 us
  matrix products: 37.7 us -> 33.3 us
    all_gather x1 -> x0, waiting for transfers between devices: 49.3 us -> none  [shards(): x = lax.all_gather(tokens, 'expert', axis=0, tiled=True)]
    ppermute x0 -> x3, waiting for transfers between devices: none -> 44.6 us  [keys_play(): ppermute(cards[-1], peer_axis, [(dev, (dev + 1) % n_parts) for dev in ran...]
    reduce_scatter x3, waiting for transfers between devices: 122 us -> 149 us  [reduced(): lax.psum_scatter(part.astype(jnp.bfloat16), 'dp', scatter_dimension=0, ti...]
    reduce_scatter x1, waiting for transfers between devices: 44.4 us -> 25.1 us  [shards(): lax.psum_scatter(row_sum.astype(jnp.bfloat16), 'expert', scatter_dimensio...]
    all_gather x1, waiting for transfers between devices: 37.2 us -> 21.1 us  [shards(): dy = lax.all_gather(cotangent, 'expert', axis=0, tiled=True)]
    unnamed x26 -> x39, local copies, waits for them, and re-layouts: 5.92 us -> 7.82 us
  transfers between devices with their start and end apart: 6 -> 8, of which waited for: 6 -> 8; matrix products, arithmetic and copies ran while one was open for 9% -> 9% of each run, Pallas kernels for 0% -> 0%
where the time goes in v1:
time: 315 us
  waiting for transfers between devices  240 us (76%)
  matrix products  33.3 us (11%)
  blocking collectives  15.8 us (5%)
  between operations  14 us (4%)
  local copies, waits for them, and re-layouts  7.85 us (2%)
  starting transfers between devices  3.49 us (1%)
    reduce_scatter x3, waiting for transfers between devices, reduced(): lax.psum_scatter(part.astype(jnp.bfloat16), 'dp', scatter_dimension=0, ti...  149 us
    ppermute x3, waiting for transfers between devices, keys_play(): ppermute(cards[-1], peer_axis, [(dev, (dev + 1) % n_parts) for dev in ran...  44.6 us
    reduce_scatter x1, waiting for transfers between devices, shards(): lax.psum_scatter(row_sum.astype(jnp.bfloat16), 'expert', scatter_dimensio...  25.1 us
    all_gather x1, waiting for transfers between devices, shards(): dy = lax.all_gather(cotangent, 'expert', axis=0, tiled=True)  21.1 us
    all_to_all x1, blocking collectives, shards(): lax.all_to_all(comb, 'expert', split_axis=1, concat_axis=0, tiled=True)  7.91 us
    all_to_all x1, blocking collectives, shards(): lax.all_to_all(weight, 'expert', split_axis=1, concat_axis=0, tiled=True)  7.9 us
    unnamed x39, local copies, waits for them, and re-layouts  7.82 us
  transfers between devices with their start and end apart: 8, of which 8 were waited for; matrix products, arithmetic and copies ran while one was open for 9% of the time, Pallas kernels for 0%

profile of v1, /device:TPU:0, one launch (start us, length us, event | category | flops | bytes accessed | tf_op | source)
XLA Modules:
  0.0 314.8 jit_solution(17597864913126749833)
XLA Ops:
  7.2 0.0 copy-start
  7.2 0.0 all-gather.2.cloned.1.call-start
  7.2 3.1 collective-permute-start
  10.3 14.2 %collective-permute-done = bf16[128,2048]{1,0:T(8,128)(2,1)S(1)} collective-permute-done((bf16[128,2048]{1,0:T(8,128)(2,1)}, bf16[128,2048]{1,0:T(8,128)(2,1)S(1)}, u32[]{:S(2)}, u32[]{:S(2)}) %collective-permute-start) | collective-permute-done | bytes 524320 | tf_op jit(solution)/shard_map/ppermute | solution.py:14
  24.5 0.8 copy-done.2
  25.3 0.0 collective-permute-start.1
  25.3 15.0 %collective-permute-done.1 = bf16[128,2048]{1,0:T(8,128)(2,1)} collective-permute-done((bf16[128,2048]{1,0:T(8,128)(2,1)S(1)}, bf16[128,2048]{1,0:T(8,128)(2,1)}, u32[]{:S(2)}, u32[]{:S(2)}) %collective-permute-start.1) | collective-permute-done | bytes 524320 | tf_op jit(solution)/shard_map/ppermute | solution.py:14
  40.3 0.0 collective-permute-start.2
  40.3 0.0 all-gather.2.cloned.1.call-update
  40.3 0.0 reduce-scatter.5.cloned.1.call-start
  40.4 0.0 copy-start.3
  40.4 15.4 %collective-permute-done.2 = bf16[128,2048]{1,0:T(8,128)(2,1)} collective-permute-done((bf16[128,2048]{1,0:T(8,128)(2,1)}, bf16[128,2048]{1,0:T(8,128)(2,1)}, u32[]{:S(2)}, u32[]{:S(2)}) %collective-permute-start.2) | collective-permute-done | bytes 524320 | tf_op jit(solution)/shard_map/ppermute | solution.py:14
  55.8 1.1 constant_dynamic-update-slice_fusion.7
  56.9 1.1 constant_dynamic-update-slice_fusion.6
  58.0 0.0 copy-start.8
  58.0 1.2 constant_dynamic-update-slice_fusion.5
  59.3 1.1 constant_dynamic-update-slice_fusion.3
  60.4 1.1 constant_dynamic-update-slice_fusion.2
  61.6 1.8 fusion.4
  63.4 0.2 copy-done.4
  63.5 1.2 copy-done.13
  64.7 3.3 %multiply_convert_fusion = (bf16[512,768]{1,0:T(8,128)(2,1)}, f32[512,768]{1,0:T(8,128)}) fusion(f32[512,768]{1,0:T(8,128)S(1)} %fusion.4, bf16[1,2048,768]{2,1,0:T(8,128)(2,1)S(1)} %copy-done, bf16[1024,2048]{1,0:T(8,128)(2,1)S(1)} %constant_dynamic-update-slice_fusion, s32[]{:T(128)S(6)} %select_n.23), kind=kOutput, calls=%fused_computation.19 | convolution fusion | flops 1612972032 | bytes 9175044 | tf_op jit(solution)/shard_map/dot_general | solution.py:44
  68.0 21.1 %all-gather.2.cloned.1.call-done = bf16[512,2048]{1,0:T(8,128)(2,1)} async-done(((bf16[128,2048]{1,0:T(8,128)(2,1)}), bf16[512,2048]{1,0:T(8,128)(2,1)}) %all-gather.2.cloned.1.call-update) | async-done | bytes 2097168 | tf_op jit(solution)/shard_map/all_gather | solution.py:38
  89.1 4.8 %fusion.1 = f32[512]{0:T(512)S(1)} fusion(bf16[512,2048]{1,0:T(8,128)(2,1)} %all-gather.2.cloned.1.call-done, bf16[512,768]{1,0:T(8,128)(2,1)} %get-tuple-element.9, bf16[1,768,2048]{2,1,0:T(8,128)(2,1)} %param.13), kind=kOutput, calls=%fused_computation.3 | convolution fusion | flops 1613757952 | bytes 6031360 | tf_op jit(solution)/shard_map/dot_general | solution.py:49
  93.9 7.9 %all_to_all.32 = f32[1,4,128]{2,0,1:T(1,128)S(1)} all-to-all(f32[1,4,128]{2,0,1:T(1,128)S(1)} %bitcast.46), channel_id=1, replica_groups=mesh['dp'=8,'expert'=4] {'expert'}, dimensions={1} | all-to-all | bytes 4096 | tf_op jit(solution)/shard_map/all_to_all | solution.py:76
  101.8 0.0 copy-done.6
  101.8 0.6 select_reduce_fusion
  102.4 7.9 %all_to_all.33 = f32[128,4,1]{0,2,1:T(1,128)S(1)} all-to-all(f32[128,4,1]{0,2,1:T(1,128)S(1)} %bitcast.43), channel_id=1, replica_groups=mesh['dp'=8,'expert'=4] {'expert'}, dimensions={1} | all-to-all | bytes 4096 | tf_op jit(solution)/shard_map/all_to_all | solution.py:36
  110.3 0.0 copy-done.10
  110.3 0.0 copy-start.9
  110.3 2.3 multiply_convert_fusion.1
  112.7 1.8 fusion.2
  114.5 0.0 copy-done.12
  114.5 3.1 add_convert_fusion
  117.7 0.0 reduce-scatter.5.cloned.1.call-update
  117.7 0.0 reduce-scatter.11.cloned.1.call-start
  117.7 5.4 %convolution_convert_fusion = bf16[768,2048]{1,0:T(8,128)(2,1)} fusion(bf16[512,768]{1,0:T(8,128)(2,1)} %get-tuple-element.9, bf16[512,2048]{1,0:T(8,128)(2,1)} %all-gather.2.cloned.1.call-done, f32[512]{0:T(512)S(1)} %bitcast.45), kind=kOutput, calls=%fused_computation.5 | convolution fusion | flops 1615331328 | bytes 6031360 | tf_op jit(solution)/shard_map/dot_general | solution.py:57
  123.2 0.0 reduce-scatter.11.cloned.1.call-update
  123.2 0.2 reduce-scatter.7.cloned.1.call-start
  123.4 5.3 %convolution_convert_fusion.2 = bf16[2048,768]{1,0:T(8,128)(2,1)} fusion(bf16[512,768]{1,0:T(8,128)(2,1)} %copy-done.12, bf16[1024,2048]{1,0:T(8,128)(2,1)} %copy-done.4, s32[]{:T(128)S(6)} %select_n.23), kind=kOutput, calls=%fused_computation.7 | convolution fusion | flops 1612185600 | bytes 6029316 | tf_op jit(solution)/shard_map/dot_general | solution.py:58
  128.7 0.0 reduce-scatter.7.cloned.1.call-update
  128.8 0.0 reduce-scatter.9.cloned.1.call-start
  128.8 5.4 %convolution_convert_fusion.1 = bf16[2048,768]{1,0:T(8,128)(2,1)} fusion(bf16[512,768]{1,0:T(8,128)(2,1)} %copy-done.11, bf16[1024,2048]{1,0:T(8,128)(2,1)} %copy-done.4, s32[]{:T(128)S(6)} %select_n.23), kind=kOutput, calls=%fused_computation.6 | convolution fusion | flops 1612185600 | bytes 6029316 | tf_op jit(solution)/shard_map/dot_general | solution.py:59
  134.2 0.0 reduce-scatter.9.cloned.1.call-update
  134.2 25.1 %reduce-scatter.5.cloned.1.call-done = bf16[128,2048]{1,0:T(8,128)(2,1)} async-done(((bf16[512,2048]{1,0:T(8,128)(2,1)}), bf16[128,2048]{1,0:T(8,128)(2,1)}) %reduce-scatter.5.cloned.1.call-update) | async-done | bytes 524304 | tf_op jit(solution)/shard_map/reduce_scatter | solution.py:72
  159.3 49.3 %reduce-scatter.11.cloned.1.call-done = bf16[96,2048]{1,0:T(8,128)(2,1)} async-done(((bf16[768,2048]{1,0:T(8,128)(2,1)}), bf16[96,2048]{1,0:T(8,128)(2,1)}) %reduce-scatter.11.cloned.1.call-update) | async-done | bytes 393232 | tf_op jit(solution)/shard_map/reduce_scatter | solution.py:64
  208.5 49.9 %reduce-scatter.7.cloned.1.call-done = bf16[256,768]{1,0:T(8,128)(2,1)} async-done(((bf16[2048,768]{1,0:T(8,128)(2,1)}), bf16[256,768]{1,0:T(8,128)(2,1)}) %reduce-scatter.7.cloned.1.call-update) | async-done | bytes 393232 | tf_op jit(solution)/shard_map/reduce_scatter | solution.py:64
  258.4 49.9 %reduce-scatter.9.cloned.1.call-done = bf16[256,768]{1,0:T(8,128)(2,1)} async-done(((bf16[2048,768]{1,0:T(8,128)(2,1)}), bf16[256,768]{1,0:T(8,128)(2,1)}) %reduce-scatter.9.cloned.1.call-update) | async-done | bytes 393232 | tf_op jit(solution)/shard_map/reduce_scatter | solution.py:64
  (25 shorter events, 0.2 us)
Async XLA Ops:
  7.2 57.5 %copy-start = (bf16[1,2048,768]{2,1,0:T(8,128)(2,1)S(1)}, bf16[1,2048,768]{2,1,0:T(8,128)(2,1)}, u32[]{:S(2)}) copy-start(bf16[1,2048,768]{2,1,0:T(8,128)(2,1)} %param.12) | copy-start | bytes 9437188
  7.2 81.9 %all-gather.2.cloned.1.call-start = ((), (), s32[]{:S(2)}) async-start(), calls=%async_computation.6 | async-start | bytes 2621440 | tf_op jit(solution)/shard_map/all_gather | solution.py:38
  7.2 17.3 %collective-permute-start = (bf16[128,2048]{1,0:T(8,128)(2,1)}, bf16[128,2048]{1,0:T(8,128)(2,1)S(1)}, u32[]{:S(2)}, u32[]{:S(2)}) collective-permute-start(bf16[128,2048]{1,0:T(8,128)(2,1)} %param.7), channel_id=1, source_target_pairs={{0,1},{1,2},{2,3},{3,0},{4,5},{5,6},{6,7},{7,4},{8,9},{9,10},{10,1... | collective-permute-start | bytes 1572872 | tf_op jit(solution)/shard_map/ppermute | solution.py:14
  24.5 0.8 copy-start.2
  25.3 15.0 %collective-permute-start.1 = (bf16[128,2048]{1,0:T(8,128)(2,1)S(1)}, bf16[128,2048]{1,0:T(8,128)(2,1)}, u32[]{:S(2)}, u32[]{:S(2)}) collective-permute-start(bf16[128,2048]{1,0:T(8,128)(2,1)S(1)} %collective-permute-done), channel_id=1, source_target_pairs={{0,1},{1,2},{2,3},{3,0},{4,5},{5,6},{6,7},{7,4},{8,9},{9,10},{10,1... | collective-permute-start | bytes 1572872 | tf_op jit(solution)/shard_map/ppermute | solution.py:14
  40.3 15.5 %collective-permute-start.2 = (bf16[128,2048]{1,0:T(8,128)(2,1)}, bf16[128,2048]{1,0:T(8,128)(2,1)}, u32[]{:S(2)}, u32[]{:S(2)}) collective-permute-start(bf16[128,2048]{1,0:T(8,128)(2,1)} %collective-permute-done.1), channel_id=1, source_target_pairs={{0,1},{1,2},{2,3},{3,0},{4,5},{5,6},{6,7},{7,4},{8,9},{9,10},{10,1... | collective-permute-start | bytes 1572872 | tf_op jit(solution)/shard_map/ppermute | solution.py:14
  40.3 119.0 %reduce-scatter.5.cloned.1.call-start = ((), (), s32[]{:S(2)}) async-start(), calls=%async_computation.7 | async-start | bytes 2621440 | tf_op jit(solution)/shard_map/reduce_scatter | solution.py:72
  40.4 18.9 %copy-start.1 = (bf16[128,2048]{1,0:T(8,128)(2,1)S(1)}, bf16[128,2048]{1,0:T(8,128)(2,1)}, u32[]{:S(2)}) copy-start(bf16[128,2048]{1,0:T(8,128)(2,1)} %param.7) | copy-start | bytes 1572868
  40.4 21.1 %copy-start.3 = (bf16[128,2048]{1,0:T(8,128)(2,1)S(1)}, bf16[128,2048]{1,0:T(8,128)(2,1)}, u32[]{:S(2)}) copy-start(bf16[128,2048]{1,0:T(8,128)(2,1)} %copy-done.2) | copy-start | bytes 1572868
  58.0 3.6 %copy-start.8 = (bf16[1,2048,768]{2,1,0:T(8,128)(2,1)S(1)}, bf16[1,2048,768]{2,1,0:T(8,128)(2,1)}, u32[]{:S(2)}) copy-start(bf16[1,2048,768]{2,1,0:T(8,128)(2,1)} %param.11) | copy-start | bytes 9437188
  61.6 2.0 copy-start.4
  63.5 1.2 copy-start.13
  89.0 12.7 %copy-start.5 = (s32[128,2]{0,1:T(2,128)S(1)}, s32[128,2]{0,1:T(2,128)}, u32[]{:S(2)}) copy-start(s32[128,2]{0,1:T(2,128)} %param.9) | copy-start | bytes 3076
  89.0 12.7 %copy-start.6 = (f32[128,2]{0,1:T(2,128)S(1)}, f32[128,2]{0,1:T(2,128)}, u32[]{:S(2)}) copy-start(f32[128,2]{0,1:T(2,128)} %param.10) | copy-start | bytes 3076
  89.1 21.2 %copy-start.7 = (bf16[1,768,2048]{2,1,0:T(8,128)(2,1)S(1)}, bf16[1,768,2048]{2,1,0:T(8,128)(2,1)}, u32[]{:S(2)}) copy-start(bf16[1,768,2048]{2,1,0:T(8,128)(2,1)} %param.13) | copy-start | bytes 9437188
  89.1 21.2 %copy-start.10 = (bf16[512,2048]{1,0:T(8,128)(2,1)S(1)}, bf16[512,2048]{1,0:T(8,128)(2,1)}, u32[]{:S(2)}) copy-start(bf16[512,2048]{1,0:T(8,128)(2,1)} %all-gather.2.cloned.1.call-done) | copy-start | bytes 6291460
  89.1 21.2 %copy-start.14 = (f32[512,768]{1,0:T(8,128)S(1)}, f32[512,768]{1,0:T(8,128)}, u32[]{:S(2)}) copy-start(f32[512,768]{1,0:T(8,128)} %copy-done.13) | copy-start | bytes 4718596
  89.1 21.2 %copy-start.15 = (f32[512,768]{1,0:T(8,128)S(1)}, f32[512,768]{1,0:T(8,128)}, u32[]{:S(2)}) copy-start(f32[512,768]{1,0:T(8,128)} %get-tuple-element.10) | copy-start | bytes 4718596
  110.3 2.4 copy-start.9
  112.6 1.9 copy-start.12
  112.7 1.9 copy-start.11
  117.7 90.9 %reduce-scatter.11.cloned.1.call-start = ((), (), s32[]{:S(2)}) async-start(), calls=%async_computation.10 | async-start | bytes 3538944 | tf_op jit(solution)/shard_map/reduce_scatter | solution.py:64
  123.2 135.2 %reduce-scatter.7.cloned.1.call-start = ((), (), s32[]{:S(2)}) async-start(), calls=%async_computation.8 | async-start | bytes 3538944 | tf_op jit(solution)/shard_map/reduce_scatter | solution.py:64
  128.8 179.5 %reduce-scatter.9.cloned.1.call-start = ((), (), s32[]{:S(2)}) async-start(), calls=%async_computation.9 | async-start | bytes 3538944 | tf_op jit(solution)/shard_map/reduce_scatter | solution.py:64
Sparse Core Ops, SparseCore 0:
  40.4 48.5 all-gather.1
  117.8 41.4 reduce-scatter.4
  163.2 45.2 reduce-scatter.10
  212.4 46.0 reduce-scatter.6
  262.2 46.0 reduce-scatter.8
